TPU v7x, 32 devices: a whole 2x2x4 slice. The times are simulated.
32 devices in a mesh: ctx: 8 (over z, core), fsdp: 4 (over y, x).
Axes of the slice: x: 2, y: 2, z: 4, core: 2. Of those that a mesh axis runs over, the one named last changes fastest.
Arguments:
- tokens: bfloat16 [4, 1024, 1024], P('fsdp', 'ctx'), may hold values from -6 to 6
- norm_first: bfloat16 [1024], P(('ctx', 'fsdp')), may hold values from 0.099609375 to 1.8984375
- w_query: bfloat16 [1024, 1024], P(('ctx', 'fsdp')), may hold values from -0.65625 to 0.65625
- w_key: bfloat16 [1024, 512], P(('ctx', 'fsdp')), may hold values from -0.65625 to 0.65625
- w_value: bfloat16 [1024, 512], P(('ctx', 'fsdp')), may hold values from -0.1875 to 0.1875
- w_out: bfloat16 [1024, 1024], P(('ctx', 'fsdp')), may hold values from -6 to 6
- norm_second: bfloat16 [1024], P(('ctx', 'fsdp')), may hold values from 0.099609375 to 1.8984375
- w_router: bfloat16 [1024, 32], P(('ctx', 'fsdp')), may hold values from -0.375 to 0.375
- w_gate: bfloat16 [32, 1024, 512], P('fsdp', 'ctx'), may hold values from -0.1875 to 0.1875
- w_up: bfloat16 [32, 1024, 512], P('fsdp', 'ctx'), may hold values from -0.1875 to 0.1875
- w_down: bfloat16 [32, 512, 1024], P('fsdp', None, 'ctx'), may hold values from -2.390625 to 2.390625
- positions: int32 [4, 1024], P('fsdp', 'ctx'), may hold values from 0 to 1023, as said below
- routes: int32 [4, 1024, 8], P('fsdp', 'ctx'), may hold values from 0 to 31, all different within a row; in each aligned block of 128 rows (0 to 127, 128 to 255, ..., all dimensions but the last counted through in order) at most 48 rows name the same one
- cotangent: bfloat16 [4, 1024, 1024], P('fsdp', 'ctx'), may hold values from -6 to 6
Outputs:
- output: bfloat16 [4, 1024, 1024], P('fsdp', 'ctx')
- grad_tokens: float32 [4, 1024, 1024], P('fsdp', 'ctx')
- grad_norm_first: float32 [1024], P(('ctx', 'fsdp'))
- grad_query: float32 [1024, 1024], P(('ctx', 'fsdp'))
- grad_key: float32 [1024, 512], P(('ctx', 'fsdp'))
- grad_value: float32 [1024, 512], P(('ctx', 'fsdp'))
- grad_out: float32 [1024, 1024], P(('ctx', 'fsdp'))
- grad_norm_second: float32 [1024], P(('ctx', 'fsdp'))
- grad_router: float32 [1024, 32], P(('ctx', 'fsdp'))
- grad_gate: float32 [32, 1024, 512], P('fsdp', 'ctx')
- grad_up: float32 [32, 1024, 512], P('fsdp', 'ctx')
- grad_down: float32 [32, 512, 1024], P('fsdp', None, 'ctx')
Inputs may be any that keep to these rules, and one draw needn't show every extreme that they name: Each sequence's positions are a permutation of 0 to 1023, made of runs of 64 consecutive increasing positions in an order drawn per sequence. `routes`: each row names 8 different experts; within the rows of one device (aligned blocks of 128 rows, sequences in order) no expert is named by more than 48 rows.
All inputs are finite; a program needn't handle non-finite values.
Results may differ from a plain program's by a relative error of at most 0.025.
The roundings to bfloat16 on the way count: a program that leaves them out, or rounds other values in their place, can miss the bound.
Values may be sent and summed in bfloat16 or wider, within the bound.
A program may use at most 192 MiB of HBM per device.

v0:
```python
import math

import jax
import jax.numpy as jnp
from jax import lax
from jax.sharding import PartitionSpec as P

D = 1024
HEADS = 16
KV_HEADS = 8
HEAD = 64
EXPERTS = 32
TOP = 8
CAP = 48


residual_scale = 0.22
score_scale = 0.015625
rope_base = 10000.0
norm_eps = 1e-06
masked_score = -1e30


def rope_tables(position, head_size):
    half_size = head_size // 2
    frequency = rope_base ** (jnp.arange(half_size, dtype=jnp.float32) * (-2.0 / head_size))
    angles = position.astype(jnp.float32)[:, None] * frequency[None, :]
    return (jnp.cos(angles)[:, None, :], jnp.sin(angles)[:, None, :])


def rotate(values_in, position):
    cosine, sine_part = rope_tables(position, values_in.shape[-1])
    half_size = values_in.shape[-1] // 2
    front_half = values_in[..., :half_size]
    back_half = values_in[..., half_size:]
    return jnp.concatenate(
        [front_half * cosine - back_half * sine_part, back_half * cosine + front_half * sine_part],
        axis=-1,
    )


def unrotate(gradient, position):
    cosine, sine_part = rope_tables(position, gradient.shape[-1])
    half_size = gradient.shape[-1] // 2
    front_half = gradient[..., :half_size]
    back_half = gradient[..., half_size:]
    return jnp.concatenate(
        [front_half * cosine + back_half * sine_part, back_half * cosine - front_half * sine_part],
        axis=-1,
    )


def norm_parts(values_in):
    inverse = lax.rsqrt(jnp.mean(values_in * values_in, axis=-1, keepdims=True) + norm_eps)
    return (values_in * inverse, inverse)


def norm_back(d_output, normalized, inverse, gain_vector):
    d_norm = d_output * gain_vector
    d_values = inverse * (
        d_norm - normalized * jnp.mean(d_norm * normalized, axis=-1, keepdims=True)
    )
    return (d_values, jnp.sum(d_output * normalized, axis=0))


def over_blocks(block_step, running, shard_piece, begin_at):
    count_rows = shard_piece[0].shape[0]
    block_size = count_rows if count_rows <= 1024 else math.gcd(count_rows, 1024)
    if block_size == count_rows:
        return block_step(running, shard_piece, begin_at)

    def inner_step(state_now, block_index):
        sub_piece = tuple(
            (
                lax.dynamic_slice_in_dim(member, block_index * block_size, block_size, 0)
                for member in shard_piece
            )
        )
        return (block_step(state_now, sub_piece, begin_at + block_index * block_size), None)

    return lax.scan(inner_step, running, jnp.arange(count_rows // block_size, dtype=jnp.int32))[0]


def local(
    tokens,
    norm_first,
    w_query,
    w_key,
    w_value,
    w_out,
    norm_second,
    w_router,
    w_gate,
    w_up,
    w_down,
    positions,
    routes,
    cotangent,
):
    gain_one, query_w, key_w, value_w, out_w, gain_two, router_w = (
        lax.all_gather(norm_first, ("ctx", "fsdp"), axis=0, tiled=True),
        lax.all_gather(w_query, ("ctx", "fsdp"), axis=0, tiled=True),
        lax.all_gather(w_key, ("ctx", "fsdp"), axis=0, tiled=True),
        lax.all_gather(w_value, ("ctx", "fsdp"), axis=0, tiled=True),
        lax.all_gather(w_out, ("ctx", "fsdp"), axis=0, tiled=True),
        lax.all_gather(norm_second, ("ctx", "fsdp"), axis=0, tiled=True),
        lax.all_gather(w_router, ("ctx", "fsdp"), axis=0, tiled=True),
    )
    gate_w, up_w, down_w = (
        lax.all_gather(w_gate, "ctx", axis=1, tiled=True),
        lax.all_gather(w_up, "ctx", axis=1, tiled=True),
        lax.all_gather(w_down, "ctx", axis=2, tiled=True),
    )
    ctx_count = lax.axis_size("ctx")
    fsdp_count = lax.axis_size("fsdp")
    local_experts = gate_w.shape[0]
    inputs = tokens[0].astype(jnp.float32)
    token_place = positions[0]
    route_ids = routes[0]
    row_count = inputs.shape[0]
    groups = HEADS // KV_HEADS
    kv_width = KV_HEADS * HEAD
    normed_one, inverse_one = norm_parts(inputs)
    hidden_one = (normed_one * gain_one).astype(jnp.bfloat16)
    queries = (
        rotate(
            jnp.dot(hidden_one, query_w, preferred_element_type=jnp.float32).reshape(
                row_count, HEADS, HEAD
            ),
            token_place,
        )
        .astype(jnp.bfloat16)
        .reshape(row_count, KV_HEADS, groups, HEAD)
    )
    key_rows = rotate(
        jnp.dot(hidden_one, key_w, preferred_element_type=jnp.float32).reshape(
            row_count, KV_HEADS, HEAD
        ),
        token_place,
    ).astype(jnp.bfloat16)
    value_rows = (
        jnp.dot(hidden_one, value_w, preferred_element_type=jnp.float32)
        .astype(jnp.bfloat16)
        .reshape(row_count, KV_HEADS, HEAD)
    )
    key_pack = (key_rows, value_rows, token_place)

    def forward_block(running, sub_piece, begin_at):
        run_max, run_total, run_sum = running
        block_keys, block_values, block_place = sub_piece
        scores = (
            jnp.einsum("tgrd,kgd->tgrk", queries, block_keys, preferred_element_type=jnp.float32)
            * score_scale
        )
        allowed = (block_place[None, :] <= token_place[:, None])[:, None, None, :]
        scores = jnp.where(allowed, scores, masked_score)
        new_max = jnp.maximum(run_max, jnp.max(scores, axis=-1))
        fading = jnp.exp(run_max - new_max)
        weights = jnp.where(allowed, jnp.exp(scores - new_max[..., None]), 0.0)
        run_total = run_total * fading + jnp.sum(weights, axis=-1)
        run_sum = run_sum * fading[..., None] + jnp.einsum(
            "tgrk,kgd->tgrd",
            weights.astype(jnp.bfloat16),
            block_values,
            preferred_element_type=jnp.float32,
        )
        return (new_max, run_total, run_sum)

    start_state = (
        jnp.full((row_count, KV_HEADS, groups), masked_score, jnp.float32),
        jnp.zeros((row_count, KV_HEADS, groups), jnp.float32),
        jnp.zeros((row_count, KV_HEADS, groups, HEAD), jnp.float32),
    )
    all_keys = (
        lax.all_gather(key_pack[0], "ctx", axis=0, tiled=True),
        lax.all_gather(key_pack[1], "ctx", axis=0, tiled=True),
        lax.all_gather(key_pack[2], "ctx", axis=0, tiled=True),
    )
    forward_state = over_blocks(forward_block, start_state, all_keys, 0)
    run_max, run_total, run_sum = forward_state
    log_total = run_max + jnp.log(run_total)
    attended_f = run_sum / run_total[..., None]
    attended = attended_f.astype(jnp.bfloat16).reshape(row_count, HEADS * HEAD)
    middle = inputs + residual_scale * jnp.dot(attended, out_w, preferred_element_type=jnp.float32)
    normed_two, inverse_two = norm_parts(middle)
    hidden_two = (normed_two * gain_two).astype(jnp.bfloat16)
    chosen = jnp.take_along_axis(
        jnp.dot(hidden_two, router_w, preferred_element_type=jnp.float32), route_ids, axis=1
    )
    gate_weights = jax.nn.softmax(chosen, axis=-1)
    pair_count = row_count * TOP
    expert_of = route_ids.reshape(-1)
    expert_ids = jnp.arange(EXPERTS, dtype=jnp.int32)
    one_hot = (expert_of[:, None] == expert_ids[None, :]).astype(jnp.int32)
    slot_of = jnp.sum((jnp.cumsum(one_hot, axis=0) - 1) * one_hot, axis=1)
    target = expert_of * CAP + slot_of
    pair_at = (
        jnp.zeros((EXPERTS * CAP,), jnp.int32)
        .at[target]
        .set(jnp.arange(pair_count, dtype=jnp.int32) + 1)
    )
    filled = (pair_at > 0)[:, None]
    pair_safe = jnp.maximum(pair_at - 1, 0)
    outgoing = jnp.where(filled, hidden_two[pair_safe // TOP], jnp.zeros((), jnp.bfloat16)).reshape(
        fsdp_count, local_experts, CAP, D
    )
    received = lax.all_to_all(outgoing, "fsdp", split_axis=0, concat_axis=0, tiled=True)
    gate_value = jnp.einsum("sejd,edf->sejf", received, gate_w, preferred_element_type=jnp.float32)
    upward = jnp.einsum("sejd,edf->sejf", received, up_w, preferred_element_type=jnp.float32)
    hidden = (jax.nn.silu(gate_value) * upward).astype(jnp.bfloat16)
    result = jnp.einsum(
        "sejf,efd->sejd", hidden, down_w, preferred_element_type=jnp.float32
    ).astype(jnp.bfloat16)
    received, gate_value, upward, result = (received, gate_value, upward, result)
    returned = lax.all_to_all(result, "fsdp", split_axis=0, concat_axis=0, tiled=True).reshape(
        EXPERTS * CAP, D
    )
    pair_rows = returned[target].reshape(row_count, TOP, D)
    mixture = jnp.sum(gate_weights[..., None] * pair_rows, axis=1)
    output_rows = middle + residual_scale * mixture
    upstream = cotangent[0].astype(jnp.float32)
    d_gate_weights = residual_scale * jnp.sum(upstream[:, None, :] * pair_rows, axis=-1)
    pair_grads = (
        (residual_scale * gate_weights[..., None] * upstream[:, None, :])
        .astype(jnp.bfloat16)
        .reshape(pair_count, D)
    )
    grad_slots = jnp.where(filled, pair_grads[pair_safe], jnp.zeros((), jnp.bfloat16)).reshape(
        fsdp_count, local_experts, CAP, D
    )
    incoming = lax.all_to_all(grad_slots, "fsdp", split_axis=0, concat_axis=0, tiled=True)
    d_hidden = jnp.einsum("sejd,efd->sejf", incoming, down_w, preferred_element_type=jnp.float32)
    sigmoid_gate = jax.nn.sigmoid(gate_value)
    activated = gate_value * sigmoid_gate
    hidden = (activated * upward).astype(jnp.bfloat16)
    grad_down_all = jnp.einsum(
        "sejf,sejd->efd", hidden, incoming, preferred_element_type=jnp.float32
    )
    d_gate = (d_hidden * upward * sigmoid_gate * (1.0 + gate_value * (1.0 - sigmoid_gate))).astype(
        jnp.bfloat16
    )
    d_up = (d_hidden * activated).astype(jnp.bfloat16)
    grad_gate_all = jnp.einsum(
        "sejd,sejf->edf", received, d_gate, preferred_element_type=jnp.float32
    )
    grad_up_all = jnp.einsum("sejd,sejf->edf", received, d_up, preferred_element_type=jnp.float32)
    slot_grads = jnp.einsum(
        "sejf,edf->sejd", d_gate, gate_w, preferred_element_type=jnp.float32
    ) + jnp.einsum("sejf,edf->sejd", d_up, up_w, preferred_element_type=jnp.float32)
    back_rows = (
        lax.all_to_all(
            slot_grads.astype(jnp.bfloat16), "fsdp", split_axis=0, concat_axis=0, tiled=True
        )
        .astype(slot_grads.dtype)
        .reshape(EXPERTS * CAP, D)
    )
    d_hidden_two = jnp.sum(back_rows[target].reshape(row_count, TOP, D), axis=1)
    grad_gate_mine, grad_up_mine, grad_down_mine = (
        lax.psum_scatter(
            grad_gate_all.astype(jnp.bfloat16), "ctx", scatter_dimension=1, tiled=True
        ).astype(jnp.float32),
        lax.psum_scatter(
            grad_up_all.astype(jnp.bfloat16), "ctx", scatter_dimension=1, tiled=True
        ).astype(jnp.float32),
        lax.psum_scatter(
            grad_down_all.astype(jnp.bfloat16), "ctx", scatter_dimension=2, tiled=True
        ).astype(jnp.float32),
    )
    d_chosen = gate_weights * (
        d_gate_weights - jnp.sum(gate_weights * d_gate_weights, axis=-1, keepdims=True)
    )
    d_logits = jnp.sum(
        jnp.where(route_ids[..., None] == expert_ids[None, None, :], d_chosen[..., None], 0.0),
        axis=1,
    )
    grad_router = jnp.dot(
        hidden_two.astype(jnp.float32).T, d_logits, precision=lax.Precision.HIGHEST
    )
    d_hidden_two = d_hidden_two + jnp.dot(
        d_logits, router_w.astype(jnp.float32).T, precision=lax.Precision.HIGHEST
    )
    d_middle_norm, grad_gain_two = norm_back(d_hidden_two, normed_two, inverse_two, gain_two)
    d_middle = upstream + d_middle_norm
    d_attended = (residual_scale * d_middle).astype(jnp.bfloat16)
    grad_out = jnp.einsum("ti,td->id", attended, d_attended, preferred_element_type=jnp.float32)
    d_mix = (
        jnp.einsum("td,id->ti", d_attended, out_w, preferred_element_type=jnp.float32)
        .astype(jnp.bfloat16)
        .reshape(row_count, KV_HEADS, groups, HEAD)
    )
    delta_rows = jnp.sum(d_mix.astype(jnp.float32) * attended_f, axis=-1)

    def backward_block(running, sub_piece, begin_at):
        d_queries, d_kv = running
        block_keys, block_values, block_place = sub_piece
        scores = (
            jnp.einsum("tgrd,kgd->tgrk", queries, block_keys, preferred_element_type=jnp.float32)
            * score_scale
        )
        allowed = (block_place[None, :] <= token_place[:, None])[:, None, None, :]
        probabilities = jnp.where(allowed, jnp.exp(scores - log_total[..., None]), 0.0)
        d_probs = jnp.einsum(
            "tgrd,kgd->tgrk", d_mix, block_values, preferred_element_type=jnp.float32
        )
        d_scores = (probabilities * (d_probs - delta_rows[..., None])).astype(jnp.bfloat16)
        d_queries = (
            d_queries
            + jnp.einsum("tgrk,kgd->tgrd", d_scores, block_keys, preferred_element_type=jnp.float32)
            * score_scale
        )
        d_keys = (
            jnp.einsum("tgrk,tgrd->kgd", d_scores, queries, preferred_element_type=jnp.float32)
            * score_scale
        )
        d_values = jnp.einsum(
            "tgrk,tgrd->kgd",
            probabilities.astype(jnp.bfloat16),
            d_mix,
            preferred_element_type=jnp.float32,
        )
        block_rows = block_keys.shape[0]
        update = jnp.concatenate(
            [d_keys.reshape(block_rows, kv_width), d_values.reshape(block_rows, kv_width)], axis=1
        )
        current = lax.dynamic_slice_in_dim(d_kv, begin_at, block_rows, 0)
        return (d_queries, lax.dynamic_update_slice_in_dim(d_kv, current + update, begin_at, 0))

    back_start = (
        jnp.zeros((row_count, KV_HEADS, groups, HEAD), jnp.float32),
        jnp.zeros((row_count * ctx_count, 2 * kv_width), jnp.float32),
    )
    back_state = over_blocks(backward_block, back_start, all_keys, 0)
    d_queries, d_kv = back_state
    d_kv_mine = lax.psum_scatter(
        d_kv.astype(jnp.bfloat16), "ctx", scatter_dimension=0, tiled=True
    ).astype(jnp.float32)
    d_query_b = (
        unrotate(d_queries.reshape(row_count, HEADS, HEAD), token_place)
        .astype(jnp.bfloat16)
        .reshape(row_count, HEADS * HEAD)
    )
    d_key_b = (
        unrotate(d_kv_mine[:, :kv_width].reshape(row_count, KV_HEADS, HEAD), token_place)
        .astype(jnp.bfloat16)
        .reshape(row_count, kv_width)
    )
    d_value_b = d_kv_mine[:, kv_width:].astype(jnp.bfloat16)
    grad_query = jnp.einsum("td,tf->df", hidden_one, d_query_b, preferred_element_type=jnp.float32)
    grad_key = jnp.einsum("td,tf->df", hidden_one, d_key_b, preferred_element_type=jnp.float32)
    grad_value = jnp.einsum("td,tf->df", hidden_one, d_value_b, preferred_element_type=jnp.float32)
    d_hidden_one = jnp.einsum("tf,df->td", d_query_b, query_w, preferred_element_type=jnp.float32)
    d_hidden_one = d_hidden_one + jnp.einsum(
        "tf,df->td", d_key_b, key_w, preferred_element_type=jnp.float32
    )
    d_hidden_one = d_hidden_one + jnp.einsum(
        "tf,df->td", d_value_b, value_w, preferred_element_type=jnp.float32
    )
    d_input_norm, grad_gain_one = norm_back(d_hidden_one, normed_one, inverse_one, gain_one)
    d_inputs = d_middle + d_input_norm
    dense_mine = (
        lax.psum_scatter(grad_gain_one, ("ctx", "fsdp"), scatter_dimension=0, tiled=True),
        lax.psum_scatter(grad_query, ("ctx", "fsdp"), scatter_dimension=0, tiled=True),
        lax.psum_scatter(grad_key, ("ctx", "fsdp"), scatter_dimension=0, tiled=True),
        lax.psum_scatter(grad_value, ("ctx", "fsdp"), scatter_dimension=0, tiled=True),
        lax.psum_scatter(grad_out, ("ctx", "fsdp"), scatter_dimension=0, tiled=True),
        lax.psum_scatter(grad_gain_two, ("ctx", "fsdp"), scatter_dimension=0, tiled=True),
        lax.psum_scatter(grad_router, ("ctx", "fsdp"), scatter_dimension=0, tiled=True),
    )
    return (
        output_rows.astype(jnp.bfloat16)[None],
        d_inputs[None],
        dense_mine[0],
        dense_mine[1],
        dense_mine[2],
        dense_mine[3],
        dense_mine[4],
        dense_mine[5],
        dense_mine[6],
        grad_gate_mine,
        grad_up_mine,
        grad_down_mine,
    )


def solution(mesh):
    in_specs = (
        P("fsdp", "ctx", None),
        P(("ctx", "fsdp")),
        P(("ctx", "fsdp"), None),
        P(("ctx", "fsdp"), None),
        P(("ctx", "fsdp"), None),
        P(("ctx", "fsdp"), None),
        P(("ctx", "fsdp")),
        P(("ctx", "fsdp"), None),
        P("fsdp", "ctx", None),
        P("fsdp", "ctx", None),
        P("fsdp", None, "ctx"),
        P("fsdp", "ctx"),
        P("fsdp", "ctx", None),
        P("fsdp", "ctx", None),
    )
    out_specs = (
        P("fsdp", "ctx", None),
        P("fsdp", "ctx", None),
        P(("ctx", "fsdp")),
        P(("ctx", "fsdp"), None),
        P(("ctx", "fsdp"), None),
        P(("ctx", "fsdp"), None),
        P(("ctx", "fsdp"), None),
        P(("ctx", "fsdp")),
        P(("ctx", "fsdp"), None),
        P("fsdp", "ctx", None),
        P("fsdp", "ctx", None),
        P("fsdp", None, "ctx"),
    )
    return jax.shard_map(local, mesh=mesh, in_specs=in_specs, out_specs=out_specs, check_vma=False)
```

profile of v0, /device:TPU:9, one launch (start us, length us, event | category | flops | bytes accessed | tf_op | source)
XLA Modules:
  0.0 1671.6 jit_solution(12878917893361322576)
XLA Ops:
  11.2 39.8 %all-reduce.5 = (bf16[1024]{0:T(1024)(128)(2,1)S(1)}, bf16[1024]{0:T(1024)(128)(2,1)S(1)}) all-reduce(bf16[1024]{0:T(1024)(128)(2,1)S(1)} %dynamic-update-slice, bf16[1024]{0:T(1024)(128)(2,1)S(1)} %dynamic-update-slice.1), channel_id=1, replica_groups=mesh['ctx'=8,'fsdp'=4] {'ctx','fsdp'}, use_global_device_ids=true, to_apply=%add | all-reduce | flops 2048 | bytes 8192
  52.9 12.6 all-gather.11.cloned.1.call-done
  69.4 51.9 %all-gather.17.cloned.1.call-done = bf16[1024,512]{1,0:T(8,128)(2,1)} async-done(((bf16[32,512]{1,0:T(8,128)(2,1)}), bf16[1024,512]{1,0:T(8,128)(2,1)}) %all-gather.17.cloned.1.call-update) | async-done | bytes 1048592 | tf_op jit(solution)/shard_map/all_gather | solution.py:104
  127.2 9.0 reduce-window.6
  136.8 4.3 scatter_custom_fusion
  141.2 9.8 all-gather
  151.0 53.7 %all_gather.48 = bf16[1024,32]{1,0:T(8,128)(2,1)S(1)} all-gather(bf16[32,32]{1,0:T(8,128)(2,1)S(1)} %copy-done.44), channel_id=1, replica_groups=mesh['ctx'=8,'fsdp'=4] {'ctx','fsdp'}, dimensions={0}, use_global_device_ids=true | all-gather | bytes 67584 | tf_op jit(solution)/shard_map/all_gather | solution.py:107
  215.7 14.6 all-gather.19.cloned.1.call-done
  230.3 6.4 fusion.126
  236.8 50.3 %all-gather.21.cloned.1.call-done = bf16[1024,1024]{1,0:T(8,128)(2,1)} async-done(((bf16[32,1024]{1,0:T(8,128)(2,1)}), bf16[1024,1024]{1,0:T(8,128)(2,1)}) %all-gather.21.cloned.1.call-update) | async-done | bytes 2097168 | tf_op jit(solution)/shard_map/all_gather | solution.py:105
  290.4 7.0 gather_fusion.4
  298.5 5.8 gather_fusion
  304.7 5.8 gather_fusion.2
  310.5 4.3 broadcast_select_fusion
  314.8 38.4 %all_to_all.20 = bf16[4,8,48,1024]{3,2,1,0:T(8,128)(2,1)S(1)} all-to-all(bf16[4,8,48,1024]{3,2,1,0:T(8,128)(2,1)S(1)} %get-tuple-element.41), channel_id=1, replica_groups=mesh['ctx'=8,'fsdp'=4] {'fsdp'}, dimensions={0} | all-to-all | bytes 6291456 | tf_op jit(solution)/shard_map/all_to_all | solution.py:207
  353.2 5.1 all-to-all-start.2
  358.2 9.6 all-gather.25.cloned.1.call-done
  367.9 6.8 fusion.4
  374.7 75.3 %all-gather.23.cloned.1.call-done = bf16[8,1024,512]{2,1,0:T(8,128)(2,1)} async-done(((bf16[8,128,512]{2,1,0:T(8,128)(2,1)}), bf16[8,1024,512]{2,1,0:T(8,128)(2,1)}) %all-gather.23.cloned.1.call-update) | async-done | bytes 8388624 | tf_op jit(solution)/shard_map/all_gather | solution.py:110
  450.0 6.8 fusion.8
  456.9 75.5 %all-gather.27.cloned.1.call-done = bf16[8,512,1024]{2,1,0:T(8,128)(2,1)} async-done(((bf16[8,512,128]{2,1,0:T(8,128)(2,1)}), bf16[8,512,1024]{2,1,0:T(8,128)(2,1)}) %all-gather.27.cloned.1.call-update) | async-done | bytes 8388624 | tf_op jit(solution)/shard_map/all_gather | solution.py:112
  532.3 11.0 fusion.32
  543.3 7.4 fusion.2
  550.7 6.2 fusion.29
  562.9 5.7 convert_bitcast_fusion
  570.6 28.0 %all-to-all-done.3 = bf16[4,8,48,1024]{3,2,1,0:T(8,128)(2,1)S(1)} async-done(((bf16[4,8,48,1024]{3,2,1,0:T(8,128)(2,1)}), bf16[4,8,48,1024]{3,2,1,0:T(8,128)(2,1)S(1)}, u32[]{:S(2)}, u32[]{:S(2)}) %all-to-all-start.3) | async-done | bytes 3145760 | tf_op jit(solution)/shard_map/all_to_all | solution.py:251
  606.2 5.3 bitcast_convert_fusion.3
  611.5 9.2 gather_fusion.3
  620.7 4.1 bitcast_reduce_fusion
  624.8 14.8 all-to-all-done.1
  639.5 5.3 gather_fusion.1
  644.9 4.4 fusion.21
  657.0 5.1 bitcast_convert_fusion.4
  662.1 5.1 fusion.1
  673.7 8.0 bitcast_convert_fusion
  681.7 12.7 copy.172
  694.4 12.3 copy.177
  708.6 7.1 bitcast_convert_fusion.2
  716.1 7.1 bitcast_convert_fusion.1
  744.9 44.1 %all-reduce.4 = (f32[1024]{0:T(1024)S(1)}, f32[1024]{0:T(1024)S(1)}) all-reduce(f32[1024]{0:T(1024)S(1)} %get-tuple-element.16, f32[1024]{0:T(1024)S(1)} %get-tuple-element.14), channel_id=4, replica_groups=mesh['ctx'=8,'fsdp'=4] {'ctx','fsdp'}, use_global_device_ids=true, to_apply=%region_20.21.clone | all-reduce | flops 2048 | bytes 16384
  791.2 11.5 reduce-scatter.30.cloned.1.call-done
  806.7 86.1 %reduce-scatter.24.cloned.1.call-done = bf16[8,128,512]{2,1,0:T(8,128)(2,1)} async-done(((bf16[8,1024,512]{2,1,0:T(8,128)(2,1)}), bf16[8,128,512]{2,1,0:T(8,128)(2,1)}) %reduce-scatter.24.cloned.1.call-update) | async-done | bytes 1048592 | tf_op jit(solution)/shard_map/reduce_scatter | solution.py:259
  895.7 87.5 %reduce-scatter.26.cloned.1.call-done = bf16[8,128,512]{2,1,0:T(8,128)(2,1)} async-done(((bf16[8,1024,512]{2,1,0:T(8,128)(2,1)}), bf16[8,128,512]{2,1,0:T(8,128)(2,1)}) %reduce-scatter.26.cloned.1.call-update) | async-done | bytes 1048592 | tf_op jit(solution)/shard_map/reduce_scatter | solution.py:262
  985.9 118.7 %reduce-scatter.22.cloned.1.call-done = f32[32,32]{1,0:T(8,128)} async-done(((f32[1024,32]{1,0:T(8,128)}), f32[32,32]{1,0:T(8,128)}) %reduce-scatter.22.cloned.1.call-update) | async-done | bytes 4112 | tf_op jit(solution)/shard_map/reduce_scatter | solution.py:367
  1104.6 143.5 %reduce-scatter.14.cloned.1.call-done = f32[32,1024]{1,0:T(8,128)} async-done(((f32[1024,1024]{1,0:T(8,128)}), f32[32,1024]{1,0:T(8,128)}) %reduce-scatter.14.cloned.1.call-update) | async-done | bytes 131088 | tf_op jit(solution)/shard_map/reduce_scatter | solution.py:362
  1248.1 142.0 %reduce-scatter.20.cloned.1.call-done = f32[32,1024]{1,0:T(8,128)} async-done(((f32[1024,1024]{1,0:T(8,128)}), f32[32,1024]{1,0:T(8,128)}) %reduce-scatter.20.cloned.1.call-update) | async-done | bytes 131088 | tf_op jit(solution)/shard_map/reduce_scatter | solution.py:365
  1390.1 137.0 %reduce-scatter.16.cloned.1.call-done = f32[32,512]{1,0:T(8,128)} async-done(((f32[1024,512]{1,0:T(8,128)}), f32[32,512]{1,0:T(8,128)}) %reduce-scatter.16.cloned.1.call-update) | async-done | bytes 65552 | tf_op jit(solution)/shard_map/reduce_scatter | solution.py:363
  1527.2 137.1 %reduce-scatter.18.cloned.1.call-done = f32[32,512]{1,0:T(8,128)} async-done(((f32[1024,512]{1,0:T(8,128)}), f32[32,512]{1,0:T(8,128)}) %reduce-scatter.18.cloned.1.call-update) | async-done | bytes 65552 | tf_op jit(solution)/shard_map/reduce_scatter | solution.py:364
  (248 shorter events, 96.4 us)
Async XLA Ops:
  7.2 114.1 %copy-start.4 = (bf16[1,128,1024]{2,1,0:T(8,128)(2,1)S(1)}, bf16[1,128,1024]{2,1,0:T(8,128)(2,1)}, u32[]{:S(2)}) copy-start(bf16[1,128,1024]{2,1,0:T(8,128)(2,1)} %param.14) | copy-start | bytes 786436
  7.2 58.4 %all-gather.11.cloned.1.call-start = ((), (), s32[]{:S(2)}) async-start(), calls=%async_computation.13 | async-start | bytes 1081344 | tf_op jit(solution)/shard_map/all_gather | solution.py:103
  7.9 113.3 %all-gather.17.cloned.1.call-start = ((), (), s32[]{:S(2)}) async-start(), calls=%async_computation.16 | async-start | bytes 1081344 | tf_op jit(solution)/shard_map/all_gather | solution.py:104
  8.7 196.4 %all-gather.15.cloned.1.call-start = ((), (), s32[]{:S(2)}) async-start(), calls=%async_computation.15 | async-start | bytes 2162688 | tf_op jit(solution)/shard_map/all_gather | solution.py:102
  9.4 199.6 %all-gather.13.cloned.1.call-start = ((), (), s32[]{:S(2)}) async-start(), calls=%async_computation.14 | async-start | bytes 1179648 | tf_op jit(solution)/shard_map/all_gather | solution.py:175
  51.0 157.1 %copy-start.33 = (f32[1024]{0:T(1024)}, f32[1024]{0:T(1024)S(1)}, u32[]{:S(2)}) copy-start(f32[1024]{0:T(1024)S(1)} %convert_element_type.181) | copy-start | bytes 12292
  52.1 156.0 %copy-start.39 = (f32[128]{0:T(128)}, f32[128]{0:T(128)S(1)}, u32[]{:S(2)}) copy-start(f32[128]{0:T(128)S(1)} %add_rsqrt_fusion.1) | copy-start | bytes 1540
  52.9 156.0 %copy-start.29 = (f32[128,32]{0,1:T(8,128)}, f32[128,32]{0,1:T(8,128)S(1)}, u32[]{:S(2)}) copy-start(f32[128,32]{0,1:T(8,128)S(1)} %get-tuple-element.42) | copy-start | bytes 49156
  52.9 156.0 %copy-start.31 = (f32[128,32]{0,1:T(8,128)}, f32[128,32]{0,1:T(8,128)S(1)}, u32[]{:S(2)}) copy-start(f32[128,32]{0,1:T(8,128)S(1)} %get-tuple-element.43) | copy-start | bytes 49156
  68.5 57.9 %copy-start.35 = (s32[1,128,8]{1,2,0:T(8,128)S(1)}, s32[1,128,8]{1,2,0:T(8,128)}, u32[]{:S(2)}) copy-start(s32[1,128,8]{1,2,0:T(8,128)} %param.26) | copy-start | bytes 12292
  69.3 71.9 %copy-start.48 = (s32[1,128]{1,0:T(1,128)S(1)}, s32[1,128]{1,0:T(1,128)}, u32[]{:S(2)}) copy-start(s32[1,128]{1,0:T(1,128)} %param.25) | copy-start | bytes 1540
  69.3 81.7 %copy-start.44 = (bf16[32,32]{1,0:T(8,128)(2,1)S(1)}, bf16[32,32]{1,0:T(8,128)(2,1)}, u32[]{:S(2)}) copy-start(bf16[32,32]{1,0:T(8,128)(2,1)} %param.21) | copy-start | bytes 6148
  69.3 161.0 %all-gather.19.cloned.1.call-start = ((), (), s32[]{:S(2)}) async-start(), calls=%async_computation.17 | async-start | bytes 1179648 | tf_op jit(solution)/shard_map/all_gather | solution.py:176
  122.8 82.1 %copy-start.25 = (bf16[1,128,1024]{2,1,0:T(8,128)(2,1)S(1)}, bf16[1,128,1024]{2,1,0:T(8,128)(2,1)}, u32[]{:S(2)}) copy-start(bf16[1,128,1024]{2,1,0:T(8,128)(2,1)} %param.27) | copy-start | bytes 786436
  123.6 163.4 %all-gather.21.cloned.1.call-start = ((), (), s32[]{:S(2)}) async-start(), calls=%async_computation.18 | async-start | bytes 2162688 | tf_op jit(solution)/shard_map/all_gather | solution.py:105
  124.2 243.6 %all-gather.25.cloned.1.call-start = ((), (), s32[]{:S(2)}) async-start(), calls=%async_computation.20 | async-start | bytes 9437184 | tf_op jit(solution)/shard_map/all_gather | solution.py:111
  125.0 325.1 %all-gather.23.cloned.1.call-start = ((), (), s32[]{:S(2)}) async-start(), calls=%async_computation.19 | async-start | bytes 9437184 | tf_op jit(solution)/shard_map/all_gather | solution.py:110
  125.7 406.6 %all-gather.27.cloned.1.call-start = ((), (), s32[]{:S(2)}) async-start(), calls=%async_computation.21 | async-start | bytes 9437184 | tf_op jit(solution)/shard_map/all_gather | solution.py:112
  136.7 68.0 %copy-start.41 = (s32[1024,1]{0,1:T(1,128)}, s32[1024,1]{0,1:T(1,128)S(1)}, u32[]{:S(2)}) copy-start(s32[1024,1]{0,1:T(1,128)S(1)} %compare_select_fusion) | copy-start | bytes 12292
  204.7 85.4 %copy-start.18 = (bf16[1024,32]{1,0:T(8,128)(2,1)}, bf16[1024,32]{1,0:T(8,128)(2,1)S(1)}, u32[]{:S(2)}) copy-start(bf16[1024,32]{1,0:T(8,128)(2,1)S(1)} %all_gather.48) | copy-start | bytes 196612
  205.0 99.4 %copy-start.14 = (f32[128,1024]{1,0:T(8,128)}, f32[128,1024]{1,0:T(8,128)S(1)}, u32[]{:S(2)}) copy-start(f32[128,1024]{1,0:T(8,128)S(1)} %bitcast_convert_fusion.5) | copy-start | bytes 1572868
  236.8 52.5 %copy-start.27 = (bf16[128,8,2,64]{0,3,2,1:T(8,128)(2,1)}, bf16[128,8,2,64]{0,3,2,1:T(8,128)(2,1)S(1)}, u32[]{:S(2)}) copy-start(bf16[128,8,2,64]{0,3,2,1:T(8,128)(2,1)S(1)} %get-tuple-element.46) | copy-start | bytes 786436
  289.2 8.2 copy-start.47
  353.2 96.9 %copy-start.1 = (bf16[4,8,48,1024]{3,2,1,0:T(8,128)(2,1)}, bf16[4,8,48,1024]{3,2,1,0:T(8,128)(2,1)S(1)}, u32[]{:S(2)}) copy-start(bf16[4,8,48,1024]{3,2,1,0:T(8,128)(2,1)S(1)} %all_to_all.20) | copy-start | bytes 9437188
  353.2 103.7 %all-to-all-start.2 = ((bf16[4,8,48,1024]{3,2,1,0:T(8,128)(2,1)}), bf16[4,8,48,1024]{3,2,1,0:T(8,128)(2,1)}, u32[]{:S(2)}, u32[]{:S(2)}) async-start(bf16[4,8,48,1024]{3,2,1,0:T(8,128)(2,1)} %get-tuple-element.40), calls=%async_computation.2 | async-start | bytes 6291456 | tf_op jit(solution)/shard_map/all_to_all | solution.py:231
  543.3 7.4 copy-start.17
  543.3 7.4 copy-start.20
  559.2 39.4 %all-to-all-start.3 = ((bf16[4,8,48,1024]{3,2,1,0:T(8,128)(2,1)}), bf16[4,8,48,1024]{3,2,1,0:T(8,128)(2,1)S(1)}, u32[]{:S(2)}, u32[]{:S(2)}) async-start(bf16[4,8,48,1024]{3,2,1,0:T(8,128)(2,1)} %copy.149), calls=%async_computation.3 | async-start | bytes 6291456 | tf_op jit(solution)/shard_map/all_to_all | solution.py:251
  570.6 33.6 %copy-start.42 = (s32[1024,1]{0,1:T(1,128)S(1)}, s32[1024,1]{0,1:T(1,128)}, u32[]{:S(2)}) copy-start(s32[1024,1]{0,1:T(1,128)} %copy-done.41) | copy-start | bytes 12292
  600.2 39.3 %all-to-all-start.1 = ((bf16[4,8,48,1024]{3,2,1,0:T(8,128)(2,1)}), bf16[4,8,48,1024]{3,2,1,0:T(8,128)(2,1)S(1)}, u32[]{:S(2)}, u32[]{:S(2)}) async-start(bf16[4,8,48,1024]{3,2,1,0:T(8,128)(2,1)} %copy.145), calls=%async_computation.1 | async-start | bytes 6291456 | tf_op jit(solution)/shard_map/all_to_all | solution.py:215
  604.0 131.7 %reduce-scatter.28.cloned.1.call-start = ((), (), s32[]{:S(2)}) async-start(), calls=%async_computation.29 | async-start | bytes 2359296
  644.9 5.4 copy-start.10
  644.9 5.4 copy-start.19
  644.9 7.1 copy-start.26
  644.9 9.9 copy-start.12
  662.1 7.2 copy-start.22
  662.1 7.2 copy-start.24
  673.4 129.2 %reduce-scatter.30.cloned.1.call-start = ((), (), s32[]{:S(2)}) async-start(), calls=%async_computation.30 | async-start | bytes 9437184
  706.8 186.1 %reduce-scatter.24.cloned.1.call-start = ((), (), s32[]{:S(2)}) async-start(), calls=%async_computation.27 | async-start | bytes 9437184 | tf_op jit(solution)/shard_map/reduce_scatter | solution.py:259
  715.8 267.3 %reduce-scatter.26.cloned.1.call-start = ((), (), s32[]{:S(2)}) async-start(), calls=%async_computation.28 | async-start | bytes 9437184 | tf_op jit(solution)/shard_map/reduce_scatter | solution.py:262
  723.3 5.7 copy-start.5
  723.3 5.7 copy-start.34
  723.3 5.7 copy-start.40
  723.3 381.3 %reduce-scatter.22.cloned.1.call-start = ((), (), s32[]{:S(2)}) async-start(), calls=%async_computation.26 | async-start | bytes 540672 | tf_op jit(solution)/shard_map/reduce_scatter | solution.py:367
  728.9 519.2 %reduce-scatter.14.cloned.1.call-start = ((), (), s32[]{:S(2)}) async-start(), calls=%async_computation.22 | async-start | bytes 4325376 | tf_op jit(solution)/shard_map/reduce_scatter | solution.py:362
  731.8 658.3 %reduce-scatter.20.cloned.1.call-start = ((), (), s32[]{:S(2)}) async-start(), calls=%async_computation.25 | async-start | bytes 4325376 | tf_op jit(solution)/shard_map/reduce_scatter | solution.py:365
  735.6 791.6 %reduce-scatter.16.cloned.1.call-start = ((), (), s32[]{:S(2)}) async-start(), calls=%async_computation.23 | async-start | bytes 2162688 | tf_op jit(solution)/shard_map/reduce_scatter | solution.py:363
  738.7 925.6 %reduce-scatter.18.cloned.1.call-start = ((), (), s32[]{:S(2)}) async-start(), calls=%async_computation.24 | async-start | bytes 2162688 | tf_op jit(solution)/shard_map/reduce_scatter | solution.py:364
  (23 other events, 56.7 us)
Sparse Core Ops, SparseCore 0:
  11.0 54.5 all-gather.10
  68.5 52.6 all-gather.16
  124.1 55.6 all-gather.14
  181.8 24.5 all-gather.12
  208.4 21.8 all-gather.18
  233.1 53.9 all-gather.20
  288.6 79.1 all-gather.24
  369.5 80.5 all-gather.22
  451.6 80.6 all-gather.26
  673.6 33.1 reduce-scatter.27
  709.0 93.5 reduce-scatter.29
  804.8 87.9 reduce-scatter.23
  895.1 87.9 reduce-scatter.25
  985.8 118.7 reduce-scatter.21
  1107.3 140.7 reduce-scatter.13
  1250.8 139.2 reduce-scatter.19
  1392.8 134.3 reduce-scatter.15
  1529.9 134.3 reduce-scatter.17
where the time goes:
time: 1700 us; the launch traced here: 1670 us
  waiting for transfers between devices  1200 us (71%)
  blocking collectives  186 us (11%)
  matrix products  113 us (7%)
  local copies, waits for them, and re-layouts  95.9 us (6%)
  other arithmetic  46.3 us (3%)
    reduce_scatter x1, waiting for transfers between devices, local(): lax.psum_scatter(grad_query, ('ctx', 'fsdp'), scatter_dimension=0, tiled=...  144 us
    reduce_scatter x1, waiting for transfers between devices, local(): lax.psum_scatter(grad_out, ('ctx', 'fsdp'), scatter_dimension=0, tiled=True)  142 us
    reduce_scatter x1, waiting for transfers between devices, local(): lax.psum_scatter(grad_value, ('ctx', 'fsdp'), scatter_dimension=0, tiled=...  137 us
    reduce_scatter x1, waiting for transfers between devices, local(): lax.psum_scatter(grad_key, ('ctx', 'fsdp'), scatter_dimension=0, tiled=True)  137 us
    reduce_scatter x1, waiting for transfers between devices, local(): lax.psum_scatter(grad_router, ('ctx', 'fsdp'), scatter_dimension=0, tiled...  119 us
    reduce_scatter x1, waiting for transfers between devices, local(): lax.psum_scatter(grad_up_all.astype(jnp.bfloat16), 'ctx', scatter_dimensi...  87.5 us
    reduce_scatter x1, waiting for transfers between devices, local(): lax.psum_scatter(grad_gate_all.astype(jnp.bfloat16), 'ctx', scatter_dimen...  86.1 us
    unnamed x2, blocking collectives  83.9 us
  transfers between devices with their start and end apart: 21, of which 17 were waited for; matrix products, arithmetic and copies ran while one was open for 11% of the time, Pallas kernels for 0%

commit v1 on v0

v1 whole, which is shorter than its diff:
```python
import collections
import functools

import jax
import jax.numpy as jnp
from jax import lax
from jax.experimental import pallas as pl
from jax.experimental.pallas import tpu as pltpu
from jax.sharding import PartitionSpec as P

D = 1024
HEADS = 16
KV_HEADS = 8
HEAD = 64
EXPERTS = 32
TOP = 8
CAP = 48
OWN = 2

residual_scale = 0.22
score_scale = 0.015625
rope_base = 10000.0
norm_eps = 1e-06
masked_score = -1e30

MESH = pl.DeviceIdType.MESH
Place = collections.namedtuple("Place", ["c", "f", "m", "s", "q", "w"])
Flow = collections.namedtuple("Flow", ["group", "src", "dst", "src_of", "dst_of"])


class Sizes:
    def __init__(self, mesh):
        self.C = mesh.shape["ctx"]
        self.F = mesh.shape["fsdp"]
        self.N = self.C * self.F
        self.per_f = EXPERTS // self.F
        self.G = self.per_f // OWN
        self.S = self.C // self.G
        self.Q = self.F * self.G
        self.q_heads = HEADS // self.C
        self.q_width = self.q_heads * HEAD
        self.width = self.q_width + 2 * HEAD
        self.share = self.C // KV_HEADS
        self.rows_w = D // self.N

    def place(self, c, f):
        m = lax.rem(c, self.G)
        return Place(c, f, m, lax.div(c, self.G), f * self.G + m, c * self.F + f)

    def count(self, group):
        return {"ctx": self.C, "fsdp": self.F, "world": self.N, "cube": self.Q}[group]

    def peer(self, group, me, k):
        if group == "ctx":
            return self.place(lax.rem(me.c + k, self.C), me.f)
        if group == "fsdp":
            return self.place(me.c, lax.rem(me.f + k, self.F))
        if group == "world":
            w = lax.rem(me.w + k, self.N)
            return self.place(lax.div(w, self.F), lax.rem(w, self.F))
        q = lax.rem(me.q + k, self.Q)
        return self.place(me.s * self.G + lax.rem(q, self.G), lax.div(q, self.G))


def block(ref, index):
    return ref.at[index] if index is not None else ref


def exchange(sizes, name, collective_id, flows, ins, outs):
    groups = {"ctx", "fsdp", "world", "cube"} & {flow.group for flow in flows}
    widest = "world" if "world" in groups else ("cube" if "cube" in groups else None)
    meet = [widest] if widest else []
    meet += [g for g in ("ctx", "fsdp") if g in groups and widest != "world"]

    def body(*refs):
        in_refs = refs[: len(ins)]
        out_refs = refs[len(ins) : len(ins) + len(outs)]
        scratch = refs[len(ins) + len(outs) :]
        sends = scratch[0 : len(flows)]
        recvs = scratch[len(flows) : 2 * len(flows)]
        own_sem = scratch[2 * len(flows)]
        bounces = list(scratch[2 * len(flows) + 1 :])
        me = sizes.place(lax.axis_index("ctx"), lax.axis_index("fsdp"))

        barrier = pltpu.get_barrier_semaphore()
        total = 0
        for g in meet:
            def greet(k, carry, g=g):
                p = sizes.peer(g, me, k)
                pl.semaphore_signal(barrier, inc=1, device_id=(p.c, p.f), device_id_type=MESH)
                return carry
            lax.fori_loop(1, sizes.count(g), greet, 0)
            total += sizes.count(g) - 1
        pl.semaphore_wait(barrier, total)

        def copy_of(j, k, to):
            flow = flows[j]
            if isinstance(flow.src, tuple):
                source = flow.dst_of(out_refs[flow.src[1]], me)
            else:
                source = flow.src_of(in_refs[flow.src], to)
            return pltpu.make_async_remote_copy(
                src_ref=source,
                dst_ref=flow.dst_of(out_refs[flow.dst], me),
                send_sem=sends[j].at[k],
                recv_sem=recvs[j].at[k],
                device_id=(to.c, to.f),
                device_id_type=MESH,
            )

        def start(j):
            def one(k, carry):
                copy_of(j, k, sizes.peer(flows[j].group, me, k)).start()
                return carry
            lax.fori_loop(1, sizes.count(flows[j].group), one, 0)

        def finish(j):
            def one(k, carry):
                flow = flows[j]
                n = sizes.count(flow.group)
                to = sizes.peer(flow.group, me, k)
                copy_of(j, k, to).wait_send()
                sender = sizes.peer(flow.group, me, n - k)
                landed = flow.dst_of(out_refs[flow.dst], sender)
                pltpu.make_async_remote_copy(
                    src_ref=landed, dst_ref=landed, send_sem=sends[j].at[k], recv_sem=recvs[j].at[k],
                    device_id=(to.c, to.f), device_id_type=MESH,
                ).wait_recv()
                return carry
            lax.fori_loop(1, sizes.count(flows[j].group), one, 0)

        own_flows = [j for j in range(len(flows)) if not isinstance(flows[j].src, tuple)]
        bounce_of = dict(zip(own_flows, bounces))
        for j in own_flows:
            start(j)
        loads = {}
        for j in own_flows:
            loads[j] = pltpu.make_async_copy(
                flows[j].src_of(in_refs[flows[j].src], me), bounce_of[j], own_sem.at[j, 0])
            loads[j].start()
        stores = {}
        for j in own_flows:
            loads[j].wait()
            stores[j] = pltpu.make_async_copy(
                bounce_of[j], flows[j].dst_of(out_refs[flows[j].dst], me), own_sem.at[j, 1])
            stores[j].start()
        done = set()
        for j in range(len(flows)):
            if isinstance(flows[j].src, tuple):
                for i in range(j):
                    if i not in done and flows[i].dst == flows[j].src[1]:
                        finish(i)
                        stores[i].wait()
                        done.add(i)
                start(j)
        for j in range(len(flows)):
            if j not in done:
                finish(j)
                if j in stores:
                    stores[j].wait()

    me0 = Place(0, 0, 0, 0, 0, 0)
    bounce_shapes = []
    for flow in flows:
        if not isinstance(flow.src, tuple):
            shape = jax.eval_shape(lambda a, flow=flow: a, ins[flow.src])
            bounce_shapes.append(pltpu.VMEM(flow_shape(flow, shape.shape), shape.dtype))
    return pl.pallas_call(
        body,
        name=name,
        out_shape=outs,
        in_specs=[pl.BlockSpec(memory_space=pl.ANY)] * len(ins),
        out_specs=[pl.BlockSpec(memory_space=pl.ANY)] * len(outs),
        scratch_shapes=[pltpu.SemaphoreType.DMA((sizes.count(f.group),)) for f in flows] * 2
        + [pltpu.SemaphoreType.DMA((len(flows), 2))]
        + bounce_shapes,
        compiler_params=pltpu.CompilerParams(collective_id=collective_id, has_side_effects=True),
    )(*ins)


def flow_shape(flow, shape):
    return flow.src_of(ShapeProbe(shape), Place(0, 0, 0, 0, 0, 0)).shape


class ShapeProbe:
    def __init__(self, shape):
        self.shape = tuple(shape)

    @property
    def at(self):
        return self

    def __getitem__(self, index):
        index = index if isinstance(index, tuple) else (index,)
        kept = []
        for i, n in enumerate(self.shape):
            if i >= len(index) or (isinstance(index[i], slice) and index[i] == slice(None)):
                kept.append(n)
            elif hasattr(index[i], "size") and not isinstance(index[i], int) and hasattr(index[i], "start"):
                kept.append(index[i].size)
        return ShapeProbe(kept)


whole = lambda ref, p: ref
at_c = lambda ref, p: ref.at[p.c]
at_f = lambda ref, p: ref.at[p.f]
at_q = lambda ref, p: ref.at[p.q]
at_w = lambda ref, p: ref.at[p.w]


def bf(x):
    return x.astype(jnp.bfloat16)


def f32(x):
    return x.astype(jnp.float32)


def dot32(spec, a, b, **kw):
    return jnp.einsum(spec, a, b, preferred_element_type=jnp.float32, **kw)


def norm_parts(x):
    inverse = lax.rsqrt(jnp.mean(x * x, axis=-1, keepdims=True) + norm_eps)
    return x * inverse, inverse


def norm_back(d_output, normalized, inverse, gain):
    g = d_output * gain
    return inverse * (g - normalized * jnp.mean(g * normalized, axis=-1, keepdims=True))


def turn(x, cosine, sine):
    a, b = x[..., : HEAD // 2], x[..., HEAD // 2 :]
    return jnp.concatenate([a * cosine - b * sine, b * cosine + a * sine], axis=-1)


def shape_of(shape, dtype=jnp.bfloat16):
    return jax.ShapeDtypeStruct(shape, dtype)


def local(z, tokens, norm_first, w_query, w_key, w_value, w_out, norm_second, w_router,
          w_gate, w_up, w_down, positions, routes, cotangent):
    C, F, N, Q, S, G = z.C, z.F, z.N, z.Q, z.S, z.G
    R = tokens.shape[1]
    L = C * R
    rs = z.rows_w
    ff = w_gate.shape[2]
    dc = D // C
    my_c = lax.axis_index("ctx")

    expert_ids = jnp.arange(EXPERTS, dtype=jnp.int32)
    named = jnp.any(routes[0][:, :, None] == expert_ids[None, None, :], axis=1)
    before = (jnp.arange(R)[:, None] > jnp.arange(R)[None, :]).astype(jnp.bfloat16)
    slot = dot32("tu,ue->te", before, named.astype(jnp.bfloat16)).astype(jnp.int32)
    slot = jnp.where(named, slot, -1)
    pick = (slot.T[:, None, :] == jnp.arange(CAP, dtype=jnp.int32)[None, :, None]).astype(jnp.bfloat16)
    pick = pick.reshape(EXPERTS * CAP, R)

    heads_q = w_query.reshape(rs, C, z.q_width)
    heads_k = jnp.repeat(w_key.reshape(rs, KV_HEADS, HEAD), z.share, axis=1)
    heads_v = jnp.repeat(w_value.reshape(rs, KV_HEADS, HEAD), z.share, axis=1)
    w_pack = jnp.concatenate([heads_q, heads_k, heads_v], axis=2).transpose(1, 0, 2)
    small = jnp.concatenate(
        [w_router, norm_first[:, None], norm_second[:, None], jnp.zeros((rs, 128 - EXPERTS - 2), jnp.bfloat16)], axis=1)
    place_pack = jnp.broadcast_to(positions[0][None, :], (8, R))
    cot_rows = bf(dot32("st,td->sd", pick, cotangent[0])).reshape(Q, OWN * CAP, D)

    own_pair = lambda ref, p: ref.at[pl.ds(p.m * OWN, OWN)]
    tok_all, pos_all, w_c, small_all, wo, wg, wu, wd, cot_in = exchange(
        z, "first_exchange", 0,
        [
            Flow("ctx", 3, 4, whole, lambda ref, p: ref.at[p.c, p.f]),
            Flow("ctx", 0, 0, whole, at_c),
            Flow("ctx", 1, 1, whole, at_c),
            Flow("world", 2, 2, at_c, at_w),
            Flow("world", 4, 3, whole, at_w),
            Flow("fsdp", ("out", 4), 4, None, lambda ref, p: ref.at[:, p.f]),
            Flow("ctx", 5, 5, own_pair, lambda ref, p: ref.at[:, p.c]),
            Flow("ctx", 6, 6, own_pair, lambda ref, p: ref.at[:, p.c]),
            Flow("ctx", 7, 7, own_pair, lambda ref, p: ref.at[:, p.c]),
            Flow("cube", 8, 8, at_q, at_q),
        ],
        [tokens[0], place_pack, w_pack, w_out, small, w_gate, w_up, w_down, cot_rows],
        [
            shape_of((C, R, D)),
            shape_of((C, 8, R), jnp.int32),
            shape_of((N, rs, z.width)),
            shape_of((N, rs, 128)),
            shape_of((C, F, rs, D)),
            shape_of((OWN, C, dc, ff)),
            shape_of((OWN, C, dc, ff)),
            shape_of((OWN, C, ff, dc)),
            shape_of((Q, OWN * CAP, D)),
        ],
    )
    w_c = w_c.reshape(D, z.width)
    small_all = small_all.reshape(D, 128)
    router = small_all[:, :EXPERTS]
    gain_one = f32(small_all[:, EXPERTS])
    gain_two = f32(small_all[:, EXPERTS + 1])
    place = pos_all[:, 0, :].reshape(L)

    x_all = f32(tok_all.reshape(L, D))
    n1_all, r1_all = norm_parts(x_all)
    h1_all = bf(n1_all * gain_one)
    qkv = jnp.dot(h1_all, w_c, preferred_element_type=jnp.float32)
    frequency = rope_base ** (jnp.arange(HEAD // 2, dtype=jnp.float32) * (-2.0 / HEAD))
    angles = place.astype(jnp.float32)[:, None] * frequency[None, :]
    cosine, sine = jnp.cos(angles), jnp.sin(angles)
    queries = bf(turn(qkv[:, : z.q_width].reshape(L, z.q_heads, HEAD), cosine[:, None], sine[:, None]))
    keys = bf(turn(qkv[:, z.q_width : z.q_width + HEAD], cosine, sine))
    values = bf(qkv[:, z.q_width + HEAD :])
    allowed = (place[None, :] <= place[:, None])[None]
    scores = jnp.where(allowed, dot32("thd,kd->htk", queries, keys) * score_scale, masked_score)
    lse = jax.nn.logsumexp(scores, axis=-1)
    probs = jnp.where(allowed, jnp.exp(scores - lse[..., None]), 0.0)
    attended_f = dot32("htk,kd->thd", probs, f32(values), precision=lax.Precision.HIGHEST)
    attended = bf(dot32("htk,kd->thd", bf(probs), values)).reshape(L, z.q_width)

    (att_in,) = exchange(
        z, "attended_exchange", 1, [Flow("ctx", 0, 0, at_c, at_c)],
        [attended.reshape(C, R, z.q_width)], [shape_of((C, R, z.q_width))])
    attended_mine = att_in.transpose(1, 0, 2).reshape(R, D)
    w_out_all = wo.reshape(D, D)
    x = f32(tokens[0])
    middle = x + residual_scale * jnp.dot(attended_mine, w_out_all, preferred_element_type=jnp.float32)
    n2, r2 = norm_parts(middle)
    h2 = bf(n2 * gain_two)
    logits = jnp.where(named, jnp.dot(h2, router, preferred_element_type=jnp.float32), masked_score)
    top = jnp.max(logits, axis=-1, keepdims=True)
    raised = jnp.where(named, jnp.exp(logits - top), 0.0)
    gates = raised / jnp.sum(raised, axis=-1, keepdims=True)

    rows = bf(dot32("st,td->sd", pick, h2)).reshape(Q, OWN * CAP, D)
    gate_slots = jnp.sum(f32(pick).reshape(EXPERTS, CAP, R) * gates.T[:, None, :], axis=-1)
    gate_slots = gate_slots.reshape(Q, OWN * CAP)
    pad_slots = lambda a: jnp.broadcast_to(jnp.pad(a, ((0, 0), (0, 128 - OWN * CAP)))[:, None, :], (Q, 8, 128))
    rows_in, gates_in = exchange(
        z, "rows_exchange", 2,
        [Flow("cube", 0, 0, at_q, at_q), Flow("cube", 1, 1, at_q, at_q)],
        [rows, pad_slots(gate_slots)], [shape_of((Q, OWN * CAP, D)), shape_of((Q, 8, 128), jnp.float32)])

    by_expert = lambda a: a.reshape(Q, OWN, CAP, -1).transpose(1, 0, 2, 3).reshape(OWN, Q * CAP, -1)
    by_source = lambda a: a.reshape(OWN, Q, CAP, -1).transpose(1, 0, 2, 3).reshape(Q, OWN * CAP, -1)
    xin = by_expert(rows_in)
    cin = f32(by_expert(cot_in))
    gin = by_expert(gates_in[:, 0, : OWN * CAP])
    wg = wg.reshape(OWN, D, ff)
    wu = wu.reshape(OWN, D, ff)
    wd = wd.transpose(0, 2, 1, 3).reshape(OWN, ff, D)
    gate = dot32("esd,edf->esf", xin, wg)
    up = dot32("esd,edf->esf", xin, wu)
    sig = jax.nn.sigmoid(gate)
    act = gate * sig
    hidden = bf(act * up)
    result = bf(dot32("esf,efd->esd", hidden, wd))
    d_gate_slots = residual_scale * jnp.sum(cin * f32(result), axis=-1, keepdims=True)
    d_result = bf(residual_scale * gin * cin)
    d_hidden = dot32("esd,efd->esf", d_result, wd)
    g_down = bf(dot32("esf,esd->efd", hidden, d_result))
    d_gate = bf(d_hidden * up * sig * (1.0 + gate * (1.0 - sig)))
    d_up = bf(d_hidden * act)
    g_gate = bf(dot32("esd,esf->edf", xin, d_gate))
    g_up = bf(dot32("esd,esf->edf", xin, d_up))
    d_rows = bf(dot32("esf,edf->esd", d_gate, wg) + dot32("esf,edf->esd", d_up, wu))

    out_in, d_in, dg_in = exchange(
        z, "return_exchange", 3,
        [Flow("cube", 0, 0, at_q, at_q), Flow("cube", 1, 1, at_q, at_q), Flow("cube", 2, 2, at_q, at_q)],
        [by_source(d_rows), by_source(result), pad_slots(by_source(d_gate_slots)[:, :, 0])],
        [shape_of((Q, OWN * CAP, D)), shape_of((Q, OWN * CAP, D)), shape_of((Q, 8, 128), jnp.float32)])
    d_in, out_in = out_in, d_in
    d_gates = jnp.sum(
        f32(pick).reshape(EXPERTS, CAP, R) * dg_in[:, 0, : OWN * CAP].reshape(EXPERTS, CAP, 1), axis=1).T
    weights = f32(pick).reshape(EXPERTS, CAP, R) * gates.T[:, None, :]
    mixture = dot32("st,sd->td", weights.reshape(EXPERTS * CAP, R), f32(out_in.reshape(EXPERTS * CAP, D)),
                    precision=lax.Precision.HIGHEST)
    output = bf(middle + residual_scale * mixture)
    d_h2 = dot32("st,sd->td", pick, d_in.reshape(EXPERTS * CAP, D))
    d_logits = gates * (d_gates - jnp.sum(gates * d_gates, axis=-1, keepdims=True))
    g_router = jnp.dot(f32(h2).T, d_logits, precision=lax.Precision.HIGHEST)
    d_h2 = d_h2 + jnp.dot(d_logits, f32(router).T, precision=lax.Precision.HIGHEST)
    g_gain_two = jnp.sum(d_h2 * n2, axis=0)
    d_middle = f32(cotangent[0]) + norm_back(d_h2, n2, r2, gain_two)
    d_attn = bf(residual_scale * d_middle)

    (d_attn_all,) = exchange(
        z, "upstream_exchange", 4, [Flow("ctx", 0, 0, whole, at_c)], [d_attn], [shape_of((C, R, D))])
    d_attn_all = d_attn_all.reshape(L, D)
    w_out_c = lax.dynamic_index_in_dim(wo, my_c, 0, keepdims=False).reshape(z.q_width, D)
    g_out = bf(dot32("ti,td->id", attended, d_attn_all))
    d_mix = bf(dot32("td,id->ti", d_attn_all, w_out_c)).reshape(L, z.q_heads, HEAD)
    delta = jnp.sum(f32(d_mix) * attended_f, axis=-1)
    d_probs = dot32("thd,kd->htk", d_mix, values)
    d_scores = bf(probs * (d_probs - delta.T[..., None]))
    d_q = dot32("htk,kd->thd", d_scores, keys) * score_scale
    d_k = dot32("htk,thd->kd", d_scores, queries) * score_scale
    d_v = dot32("htk,thd->kd", bf(probs), d_mix)
    d_qkv = jnp.concatenate(
        [bf(turn(d_q, cosine[:, None], -sine[:, None])).reshape(L, z.q_width), bf(turn(d_k, cosine, -sine)), bf(d_v)], axis=1)
    g_c = bf(dot32("td,tf->df", h1_all, d_qkv))
    d_h1_part = dot32("tf,df->td", d_qkv, w_c)
    g_gain_one = jnp.sum(d_h1_part * n1_all, axis=0)
    g_small = jnp.concatenate(
        [g_router, g_gain_one[:, None], g_gain_two[:, None], jnp.zeros((D, 128 - EXPERTS - 2), jnp.float32)], axis=1)

    to_set = lambda ref, p: ref.at[p.s, pl.ds(p.m * OWN, OWN)]
    from_c = lambda ref, p: ref.at[:, p.c]
    dh_in, gc_in, go_in, gs_in, gg_in, gu_in, gd_in = exchange(
        z, "last_exchange", 5,
        [
            Flow("ctx", 0, 0, at_c, at_c),
            Flow("world", 1, 1, at_w, at_w),
            Flow("fsdp", 2, 2, at_f, at_f),
            Flow("world", 3, 3, at_w, at_w),
            Flow("ctx", 4, 4, from_c, to_set),
            Flow("ctx", 5, 5, from_c, to_set),
            Flow("ctx", 6, 6, from_c, to_set),
        ],
        [
            bf(d_h1_part).reshape(C, R, D),
            g_c.reshape(N, rs, z.width),
            g_out.reshape(F, rs, D),
            g_small.reshape(N, rs, 128),
            g_gate.reshape(OWN, C, dc, ff),
            g_up.reshape(OWN, C, dc, ff),
            g_down.reshape(OWN, ff, C, dc).transpose(0, 2, 1, 3),
        ],
        [
            shape_of((C, R, D)),
            shape_of((N, rs, z.width)),
            shape_of((F, rs, D)),
            shape_of((N, rs, 128), jnp.float32),
            shape_of((S, z.per_f, dc, ff)),
            shape_of((S, z.per_f, dc, ff)),
            shape_of((S, z.per_f, ff, dc)),
        ],
    )
    d_h1 = jnp.sum(f32(dh_in), axis=0)
    n1, r1 = norm_parts(x)
    grad_tokens = d_middle + norm_back(d_h1, n1, r1, gain_one)
    gc = jnp.sum(f32(gc_in).reshape(C, F, rs, z.width), axis=1)
    join = lambda a: a.reshape(KV_HEADS, z.share, rs, HEAD).sum(axis=1).transpose(1, 0, 2).reshape(rs, KV_HEADS * HEAD)
    gs = jnp.sum(gs_in, axis=0)
    return (
        output[None],
        grad_tokens[None],
        gs[:, EXPERTS],
        gc[:, :, : z.q_width].transpose(1, 0, 2).reshape(rs, D),
        join(gc[:, :, z.q_width : z.q_width + HEAD]),
        join(gc[:, :, z.q_width + HEAD :]),
        jnp.sum(f32(go_in), axis=0),
        gs[:, EXPERTS + 1],
        gs[:, :EXPERTS],
        jnp.sum(f32(gg_in), axis=0),
        jnp.sum(f32(gu_in), axis=0),
        jnp.sum(f32(gd_in), axis=0),
    )


def solution(mesh):
    row = P(("ctx", "fsdp"), None)
    vec = P(("ctx", "fsdp"))
    seq = P("fsdp", "ctx", None)
    down = P("fsdp", None, "ctx")
    return jax.shard_map(
        functools.partial(local, Sizes(mesh)),
        mesh=mesh,
        in_specs=(seq, vec, row, row, row, row, vec, row, seq, seq, down, P("fsdp", "ctx"), seq, seq),
        out_specs=(seq, seq, vec, row, row, row, row, vec, row, seq, seq, down),
        check_vma=False,
    )
```

time: 1700 us -> 825 us (0.49); the launches traced: 1670 us -> 814 us
  waiting for transfers between devices: 1200 us -> 0 us
  Pallas kernels: 0 us -> 621 us
  blocking collectives: 186 us -> 0 us
  local copies, waits for them, and re-layouts: 95.9 us -> 58.1 us
  matrix products: 113 us -> 91.6 us
    reduce_scatter x7 -> x0, waiting for transfers between devices: 852 us -> none  [the longest x1 144 us: local(): lax.psum_scatter(grad_query, ('ctx', 'fsdp'), scatter_dimension=0, tiled=...]
    pallas_call x0 -> x6, Pallas kernels: none -> 621 us  [exchange(): pl.pallas_call(body, name=name, out_shape=outs, in_specs=[pl.BlockSpec(me...]
    all_gather x9 -> x0, waiting for transfers between devices: 290 us -> none  [the longest x1 75.5 us: local(): lax.all_gather(w_down, 'ctx', axis=2, tiled=True)]
    unnamed x2 -> x0, blocking collectives: 83.9 us -> none
    all_gather x2 -> x0, blocking collectives: 63.5 us -> none  [the longest x1 53.7 us: local(): lax.all_gather(w_router, ('ctx', 'fsdp'), axis=0, tiled=True)]
    all_to_all x3 -> x0, waiting for transfers between devices: 42.8 us -> none  [the longest x1 28 us: local(): lax.all_to_all(slot_grads.astype(jnp.bfloat16), 'fsdp', split_axis=0, con...]
    unnamed x113 -> x135, local copies, waits for them, and re-layouts: 44.7 us -> 4.56 us
    all_to_all x1 -> x0, blocking collectives: 38.4 us -> none  [local(): lax.all_to_all(outgoing, 'fsdp', split_axis=0, concat_axis=0, tiled=True)]
  transfers between devices with their start and end apart: 21 -> 0, of which waited for: 17 -> 0; matrix products, arithmetic and copies ran while one was open for 11% -> 0% of each run, Pallas kernels for 0% -> 0%
where the time goes in v1:
time: 825 us; the launch traced here: 814 us
  Pallas kernels  621 us (75%)
  matrix products  91.6 us (11%)
  local copies, waits for them, and re-layouts  58.1 us (7%)
  other arithmetic  41.1 us (5%)
    pallas_call x6, Pallas kernels, exchange(): pl.pallas_call(body, name=name, out_shape=outs, in_specs=[pl.BlockSpec(me...  621 us
    dot_general x25, matrix products, dot32(): return jnp.einsum(spec, a, b, preferred_element_type=jnp.float32, **kw)  83.5 us

profile of v1, /device:TPU:9, one launch (start us, length us, event | category | flops | bytes accessed | tf_op | source)
XLA Modules:
  0.0 813.9 jit_solution(9550848766145305116)
XLA Ops:
  11.8 3.7 convolution_convert_fusion.1
  15.5 217.8 %first_exchange.1 = (bf16[8,128,1024]{2,1,0:T(8,128)(2,1)}, s32[8,8,128]{2,1,0:T(8,128)}, bf16[32,32,256]{2,1,0:T(8,128)(2,1)}, bf16[32,32,128]{2,1,0:T(8,128)(2...) custom-call(bf16[128,1024]{1,0:T(8,128)(2,1)} %bitcast.263, ...), custom_call_target="tpu_custom_call" | custom-call | tf_op jit(solution)/shard_map/first_exchange/pallas_call | solution.py:168
  234.2 2.2 multiply_reduce_fusion.1
  237.0 1.7 constant_dynamic-slice_fusion
  238.7 1.6 broadcast_compare_fusion
  243.3 1.8 fusion.81
  247.4 4.0 copy.185
  251.5 2.6 convert_bitcast_fusion
  254.1 3.3 copy.184
  257.4 1.9 fusion.2
  259.3 2.0 exponential_reduce_fusion
  262.5 3.9 convolution_convert_fusion.9
  267.4 9.7 %attended_exchange.1 = bf16[8,128,128]{2,1,0:T(8,128)(2,1)} custom-call(bf16[8,128,128]{2,1,0:T(8,128)(2,1)} %copy.180.refs_0_), custom_call_target="tpu_custom_call" | custom-call | tf_op jit(solution)/shard_map/attended_exchange/pallas_call | solution.py:168
  277.0 1.8 copy.181
  278.8 2.3 multiply_reduce_fusion.4
  284.1 2.4 fusion.29
  289.2 3.5 convolution_convert_fusion
  292.7 46.5 %rows_exchange.1 = (bf16[16,96,1024]{2,1,0:T(8,128)(2,1)}, f32[16,8,128]{2,1,0:T(8,128)}) custom-call(bf16[16,96,1024]{2,1,0:T(8,128)(2,1)} %bitcast.254, f32[16,8,128]{2,1,0:T(8,128)} %broadcast_in_dim.119.refs_1_), custom_call_target="tpu_custom_call" | custom-call | tf_op jit(solution)/shard_map/rows_exchange/pallas_call | solution.py:168
  340.7 4.0 copy.187
  348.8 4.5 fusion.82
  353.3 3.7 multiply_convert_fusion.2
  357.0 2.7 fusion.4
  359.8 7.6 multiply_convert_fusion.3
  367.9 2.1 copy.190
  375.5 5.5 convolution_convert_fusion.3
  381.0 3.9 copy.202
  384.9 4.1 copy.203
  389.1 5.7 convolution_convert_fusion.4
  394.7 3.2 convolution_convert_fusion.5
  397.9 1.8 fusion.83
  399.9 1.8 add_convert_fusion
  401.8 2.0 copy.188
  403.7 88.8 %return_exchange.1 = (bf16[16,96,1024]{2,1,0:T(8,128)(2,1)}, bf16[16,96,1024]{2,1,0:T(8,128)(2,1)}, f32[16,8,128]{2,1,0:T(8,128)}) custom-call(bf16[16,96,1024]{2,1,0:T(8,128)(2,1)} %bitcast.253, bf16[16,96,1024]{2,1,0:T(8,128)(2,1)} %bitcast.251, f32[16,8,128]{2,1,0:T(8,128)} %broadcast_in_dim.120.refs_2_), custom_call_target="tpu_custom_call" | custom-call | tf_op jit(solution)/shard_map/return_exchange/pallas_call | solution.py:168
  492.5 4.4 fusion.14
  501.5 1.9 fusion.62
  504.6 2.7 multiply_reduce_fusion.2
  509.4 49.1 %upstream_exchange.1 = bf16[8,128,1024]{2,1,0:T(8,128)(2,1)} custom-call(bf16[128,1024]{1,0:T(8,128)(2,1)} %multiply_convert_fusion.5.refs_0_), custom_call_target="tpu_custom_call" | custom-call | tf_op jit(solution)/shard_map/upstream_exchange/pallas_call | solution.py:168
  558.5 3.0 convolution_convert_fusion.7
  561.5 2.6 convolution_convert_fusion.8
  564.1 8.4 %fusion.16 = f32[1024,2]{0,1:T(2,128)S(1)} fusion(f32[1024,1024,2]{1,0,2:T(8,128)} %copy-done.2, f32[2,1024]{1,0:T(2,128)S(1)} %copy-done.53, pred[1024,1024]{0,1:T(8,128)(4,1)S(1)} %copy-done.8, bf16[1024,2,64]{0,2,1:T(8,128)(2,1)S(1)} %bitcast.299, f32[1024,256]{0,1:T(8,128)S(1)} %copy-done.10), kind=kOutput, calls=%fused_computation.54 | convolution fusion | flops 1619392512 | bytes 9846784 | tf_op jit(solution)/shard_map/htk,kd->thd/dot_general | solution.py:220
  572.6 3.0 fusion.17
  575.6 3.5 fusion.1
  582.2 2.7 multiply_reduce_fusion
  584.9 1.6 convolution_convert_fusion.6
  588.0 209.1 %last_exchange.1 = (bf16[8,128,1024]{2,1,0:T(8,128)(2,1)}, bf16[32,32,256]{2,1,0:T(8,128)(2,1)}, bf16[4,32,1024]{2,1,0:T(8,128)(2,1)}, f32[32,32,128]{2,1,0:T(8,...) custom-call(bf16[8,128,1024]{2,1,0:T(8,128)(2,1)} %bitcast.283, ...), custom_call_target="tpu_custom_call" | custom-call | tf_op jit(solution)/shard_map/last_exchange/pallas_call | solution.py:168
  797.2 2.1 convert_reduce_fusion.3
  804.5 3.5 convert_reduce_fusion
  808.0 5.5 convert_reduce_fusion.1
  (217 shorter events, 54.9 us)
Async XLA Ops:
  0.6 7.6 copy-start
  0.7 244.5 %copy-start.59 = (f32[32]{0:T(128)}, f32[32]{0:T(128)S(1)}, u32[]{:S(2)}) copy-start(f32[32]{0:T(128)S(1)} %multiply_power_fusion) | copy-start | bytes 388
  3.8 4.3 copy-start.40
  8.1 225.3 %copy-start.39 = (s32[32,128]{1,0:T(8,128)}, s32[32,128]{1,0:T(8,128)S(1)}, u32[]{:S(2)}) copy-start(s32[32,128]{1,0:T(8,128)S(1)} %fusion.18) | copy-start | bytes 49156
  11.8 221.5 %copy-start.21 = (pred[32,48,128]{2,1,0:T(8,128)(4,1)}, pred[32,48,128]{2,1,0:T(8,128)(4,1)S(1)}, u32[]{:S(2)}) copy-start(pred[32,48,128]{2,1,0:T(8,128)(4,1)S(1)} %iota_compare_fusion) | copy-start | bytes 589828
  233.4 6.9 copy-start.6
  234.2 11.0 %copy-start.47 = (f32[1024]{0:T(1024)}, f32[1024]{0:T(1024)S(1)}, u32[]{:S(2)}) copy-start(f32[1024]{0:T(1024)S(1)} %convert_element_type.212) | copy-start | bytes 12292
  234.2 8.5 %copy-start.3 = (bf16[8,128,1024]{2,1,0:T(8,128)(2,1)S(1)}, bf16[8,128,1024]{2,1,0:T(8,128)(2,1)}, u32[]{:S(2)}) copy-start(bf16[8,128,1024]{2,1,0:T(8,128)(2,1)} %get-tuple-element.33) | copy-start | bytes 6291460
  242.5 38.6 %copy-start.42 = (f32[1024,1]{0,1:T(1,128)}, f32[1024,1]{0,1:T(1,128)S(1)}, u32[]{:S(2)}) copy-start(f32[1024,1]{0,1:T(1,128)S(1)} %copy.224) | copy-start | bytes 12292
  247.3 10.1 %copy-start.34 = (bf16[1024,32]{0,1:T(8,128)(2,1)}, bf16[1024,32]{0,1:T(8,128)(2,1)S(1)}, u32[]{:S(2)}) copy-start(bf16[1024,32]{0,1:T(8,128)(2,1)S(1)} %get-tuple-element.81) | copy-start | bytes 196612
  247.3 10.1 %copy-start.36 = (bf16[1024,32]{0,1:T(8,128)(2,1)}, bf16[1024,32]{0,1:T(8,128)(2,1)S(1)}, u32[]{:S(2)}) copy-start(bf16[1024,32]{0,1:T(8,128)(2,1)S(1)} %get-tuple-element.82) | copy-start | bytes 196612
  247.4 10.0 %copy-start.29 = (bf16[1024,2,32]{0,2,1:T(8,128)(2,1)}, bf16[1024,2,32]{0,2,1:T(8,128)(2,1)S(1)}, u32[]{:S(2)}) copy-start(bf16[1024,2,32]{0,2,1:T(8,128)(2,1)S(1)} %get-tuple-element.69) | copy-start | bytes 393220
  247.4 10.0 %copy-start.31 = (bf16[1024,2,32]{0,2,1:T(8,128)(2,1)}, bf16[1024,2,32]{0,2,1:T(8,128)(2,1)S(1)}, u32[]{:S(2)}) copy-start(bf16[1024,2,32]{0,2,1:T(8,128)(2,1)S(1)} %get-tuple-element.70) | copy-start | bytes 393220
  254.1 3.3 copy-start.7
  259.3 3.2 copy-start.2
  262.5 3.9 copy-start.52
  262.5 16.3 %copy-start.5 = (bf16[1,128,1024]{2,1,0:T(8,128)(2,1)S(1)}, bf16[1,128,1024]{2,1,0:T(8,128)(2,1)}, u32[]{:S(2)}) copy-start(bf16[1,128,1024]{2,1,0:T(8,128)(2,1)} %param.14) | copy-start | bytes 786436
  266.4 14.7 %copy-start.25 = (bf16[64,2,1024]{2,0,1:T(8,128)(2,1)}, bf16[64,2,1024]{2,0,1:T(8,128)(2,1)S(1)}, u32[]{:S(2)}) copy-start(bf16[64,2,1024]{2,0,1:T(8,128)(2,1)S(1)} %convolution_convert_fusion.9) | copy-start | bytes 786436
  282.2 4.3 copy-start.50
  348.8 4.5 copy-start.12
  348.8 4.5 copy-start.16
  348.8 8.2 %slice-start = ((s8[6291456]{0:T(1024)(128)(4,1)}), s8[4194304]{0:T(1024)(128)(4,1)S(1)}, s32[]{:S(2)}) async-start(s8[6291456]{0:T(1024)(128)(4,1)} %bitcast.246), calls=%async_computation | async-start | bytes 8388608
  353.3 3.7 slice-start.1
  353.3 3.7 copy-start.4
  353.3 3.7 copy-start.49
  357.0 2.8 copy-start.24
  359.8 7.6 copy-start.11
  389.0 5.7 copy-start.13
  389.0 5.7 copy-start.23
  394.7 3.2 copy-start.18
  501.5 5.8 copy-start.14
  501.5 5.8 copy-start.43
  501.5 5.8 copy-start.55
  558.5 5.6 copy-start.8
  558.5 5.6 copy-start.10
  558.5 5.6 copy-start.53
  561.5 11.0 %slice-start.2 = ((s8[8388608]{0:T(1024)(128)(4,1)}), s8[4194304]{0:T(1024)(128)(4,1)S(1)}, s32[]{:S(2)}) async-start(s8[8388608]{0:T(1024)(128)(4,1)} %bitcast.257), calls=%async_computation.2 | async-start | bytes 8388608
  564.1 8.5 %slice-start.3 = ((s8[8388608]{0:T(1024)(128)(4,1)}), s8[4194304]{0:T(1024)(128)(4,1)S(1)}, s32[]{:S(2)}) async-start(s8[8388608]{0:T(1024)(128)(4,1)} %bitcast.257), calls=%async_computation.3 | async-start | bytes 8388608
  575.6 3.5 copy-start.30
  575.6 3.5 copy-start.32
  588.0 211.2 %copy-start.58 = (f32[128]{0:T(128)S(1)}, f32[128]{0:T(128)}, u32[]{:S(2)}) copy-start(f32[128]{0:T(128)} %add_rsqrt_fusion.1) | copy-start | bytes 1540
  797.1 2.4 copy-start.15
  797.1 2.4 copy-start.44
  797.1 3.5 copy-start.28
  797.1 4.2 copy-start.38
  797.1 4.9 copy-start.27
  800.7 7.3 copy-start.41
  804.5 9.0 %copy-start.1 = (bf16[32,1024]{1,0:T(8,128)(2,1)S(1)}, bf16[32,1024]{1,0:T(8,128)(2,1)}, u32[]{:S(2)}) copy-start(bf16[32,1024]{1,0:T(8,128)(2,1)} %param.16) | copy-start | bytes 196612
  (18 other events, 27.5 us)
